TPU v7x, 8 devices: a whole 2x2x1 slice. The times are simulated.
8 devices in a mesh: batch: 1 (over z), row: 2 (over y), col: 4 (over x, core).
Axes of the slice: x: 2, y: 2, z: 1, core: 2. Of those that a mesh axis runs over, the one named last changes fastest.
Arguments:
- lower_mat: bfloat16 [4096, 4096], P('row', 'col')
- rhs_mat: bfloat16 [4096, 512], P('row', ('batch', 'col'))
Outputs:
- output: bfloat16 [4096, 512], P('row', ('batch', 'col'))
All inputs are finite; a program needn't handle non-finite values.
Results may differ from a plain program's by a relative error of at most 0.001.
Values are sent between devices in bfloat16 or wider.
A program may use at most 1 GiB of HBM per device.

v0:
```python
import jax
import jax.numpy as jnp
from jax import lax
from jax.sharding import PartitionSpec as P

BLOCK_SIZE = 256


def solution(mesh):
    grid_rows = mesh.shape["row"]
    grid_cols = mesh.shape["col"]

    def local_product(lower_loc, rhs_loc):
        rows_loc = lower_loc.shape[0]
        rhs_cols = rhs_loc.shape[1]
        row_blocks = rows_loc // BLOCK_SIZE
        col_blocks = lower_loc.shape[1] // BLOCK_SIZE
        gathered_rhs = lax.all_gather(rhs_loc, "row", axis=0)
        rhs_steps = gathered_rhs.reshape(grid_rows, row_blocks, BLOCK_SIZE, rhs_cols).transpose(1, 0, 2, 3).reshape(col_blocks, grid_cols * BLOCK_SIZE, rhs_cols)
        block_sum = jnp.zeros((rows_loc, rhs_cols), jnp.float32)
        for step in range(col_blocks):
            first_row = (step * grid_cols // grid_rows) * BLOCK_SIZE
            panel = lower_loc[first_row:, step * BLOCK_SIZE:(step + 1) * BLOCK_SIZE]
            panels = lax.all_gather(panel, "col", axis=1, tiled=True)
            update = jnp.dot(panels, rhs_steps[step], preferred_element_type=jnp.float32)
            block_sum = lax.dynamic_update_slice(block_sum, block_sum[first_row:] + update, (first_row, 0))
        return block_sum.astype(jnp.bfloat16)

    return jax.shard_map(local_product, mesh=mesh, in_specs=(P("row", "col"), P("row", ("batch", "col"))), out_specs=P("row", ("batch", "col")), check_vma=False)
```

profile of v0, /device:TPU:1, one launch (start us, length us, event | category | flops | bytes accessed | tf_op | source)
XLA Modules:
  0.0 135.8 jit_solution(4039091560472900919)
XLA Ops:
  6.5 0.0 all-gather.15.cloned.1.call-start
  6.5 0.7 all-gather.15.cloned.1.call-update
  7.3 0.0 all-gather.7.cloned.1.call-start
  7.3 2.3 %slice.39 = bf16[2048,256]{1,0:T(8,128)(2,1)} slice(bf16[2048,1024]{1,0:T(8,128)(2,1)} %param.2), slice={[0:2048], [0:256]} | slice | bytes 2097152 | tf_op jit(solution)/shard_map/slice | solution.py:23
  9.6 0.0 all-gather.7.cloned.1.call-update
  9.6 0.0 all-gather.9.cloned.1.call-start
  9.7 2.1 %slice.42 = bf16[1536,256]{1,0:T(8,128)(2,1)} slice(bf16[2048,1024]{1,0:T(8,128)(2,1)} %param.2), slice={[512:2048], [256:512]} | slice | bytes 1572864 | tf_op jit(solution)/shard_map/slice | solution.py:23
  11.8 0.0 all-gather.9.cloned.1.call-update
  11.8 0.0 all-gather.11.cloned.1.call-start
  11.9 1.9 %slice.45 = bf16[1024,256]{1,0:T(8,128)(2,1)} slice(bf16[2048,1024]{1,0:T(8,128)(2,1)} %param.2), slice={[1024:2048], [512:768]} | slice | bytes 1048576 | tf_op jit(solution)/shard_map/slice | solution.py:23
  13.8 0.0 all-gather.11.cloned.1.call-update
  13.8 0.0 all-gather.13.cloned.1.call-start
  13.8 1.7 %slice.48 = bf16[512,256]{1,0:T(8,128)(2,1)} slice(bf16[2048,1024]{1,0:T(8,128)(2,1)} %param.2), slice={[1536:2048], [768:1024]} | slice | bytes 524288 | tf_op jit(solution)/shard_map/slice | solution.py:23
  15.5 0.0 all-gather.13.cloned.1.call-update
  15.5 13.2 %all-gather.15.cloned.1.call-done = bf16[4096,128]{1,0:T(8,128)(2,1)} async-done(((bf16[2048,128]{1,0:T(8,128)(2,1)}), bf16[4096,128]{1,0:T(8,128)(2,1)}) %all-gather.15.cloned.1.call-update) | async-done | bytes 1048592 | tf_op jit(solution)/shard_map/all_gather | solution.py:18
  28.7 1.3 fusion.1
  30.1 32.9 %all-gather.7.cloned.1.call-done = bf16[2048,1024]{1,0:T(8,128)(2,1)} async-done(((bf16[2048,256]{1,0:T(8,128)(2,1)}), bf16[2048,1024]{1,0:T(8,128)(2,1)}) %all-gather.7.cloned.1.call-update) | async-done | bytes 4194320 | tf_op jit(solution)/shard_map/all_gather | solution.py:24
  63.0 3.4 %fusion.2 = f32[2048,128]{1,0:T(8,128)S(1)} fusion(bf16[2048,1024]{1,0:T(8,128)(2,1)} %all-gather.7.cloned.1.call-done, bf16[1024,128]{1,0:T(8,128)(2,1)S(1)} %bitcast.19), kind=kOutput, calls=%fused_computation.7 | convolution fusion | flops 536870912 | bytes 5505024 | tf_op jit(solution)/shard_map/dot_general | solution.py:25
  66.4 24.0 %all-gather.9.cloned.1.call-done = bf16[1536,1024]{1,0:T(8,128)(2,1)} async-done(((bf16[1536,256]{1,0:T(8,128)(2,1)}), bf16[1536,1024]{1,0:T(8,128)(2,1)}) %all-gather.9.cloned.1.call-update) | async-done | bytes 3145744 | tf_op jit(solution)/shard_map/all_gather | solution.py:24
  90.4 2.9 %convolution_add_fusion = f32[1536,128]{1,0:T(8,128)S(1)} fusion(bf16[1536,1024]{1,0:T(8,128)(2,1)} %all-gather.9.cloned.1.call-done, bf16[1024,128]{1,0:T(8,128)(2,1)S(1)} %bitcast.16, f32[2048,128]{1,0:T(8,128)S(1)} %fusion.2), kind=kOutput, calls=%fused_computation | convolution fusion | flops 402849792 | bytes 4980736 | tf_op jit(solution)/shard_map/dot_general | solution.py:25
  93.2 0.1 constant_dynamic-update-slice_fusion.1
  93.3 18.3 %all-gather.11.cloned.1.call-done = bf16[1024,1024]{1,0:T(8,128)(2,1)} async-done(((bf16[1024,256]{1,0:T(8,128)(2,1)}), bf16[1024,1024]{1,0:T(8,128)(2,1)}) %all-gather.11.cloned.1.call-update) | async-done | bytes 2097168 | tf_op jit(solution)/shard_map/all_gather | solution.py:24
  111.6 2.3 %constant_dynamic-update-slice_fusion = (f32[2048,128]{1,0:T(8,128)S(1)}, f32[1024,128]{1,0:T(8,128)S(1)}) fusion(f32[2048,128]{1,0:T(8,128)S(1)} %constant_dynamic-update-slice_fusion.1, bf16[1024,1024]{1,0:T(8,128)(2,1)} %all-gather.11.cloned.1.call-done, bf16[1024,128]{1,0:T(8,128)(2,1)S(1)} %bitcast.18, f32[1536,128]{1,0:T(8,128)S(1)} %convolution_add_fusion), kind=kOutput, calls=%fused_computation.4 | convolution fusion | flops 268566528 | bytes 3932160 | tf_op jit(solution)/shard_map/dot_general | solution.py:25
  113.9 12.9 %all-gather.13.cloned.1.call-done = bf16[512,1024]{1,0:T(8,128)(2,1)} async-done(((bf16[512,256]{1,0:T(8,128)(2,1)}), bf16[512,1024]{1,0:T(8,128)(2,1)}) %all-gather.13.cloned.1.call-update) | async-done | bytes 1048592 | tf_op jit(solution)/shard_map/all_gather | solution.py:24
  126.8 1.7 %fusion = f32[2048,128]{1,0:T(8,128)S(1)} fusion(f32[2048,128]{1,0:T(8,128)S(1)} %get-tuple-element.9, bf16[512,1024]{1,0:T(8,128)(2,1)} %all-gather.13.cloned.1.call-done, bf16[1024,128]{1,0:T(8,128)(2,1)S(1)} %bitcast.15, f32[1024,128]{1,0:T(8,128)S(1)} %get-tuple-element.10), kind=kOutput, calls=%fused_computation.3 | convolution fusion | flops 134283264 | bytes 1835008 | tf_op jit(solution)/shard_map/dot_general | solution.py:25
  128.5 0.8 convert_element_type.3
  (4 shorter events, 0.1 us)
Async XLA Ops:
  6.5 22.2 %all-gather.15.cloned.1.call-start = ((), (), s32[]{:S(2)}) async-start(), calls=%async_computation.4 | async-start | bytes 1572864 | tf_op jit(solution)/shard_map/all_gather | solution.py:18
  7.3 55.7 %all-gather.7.cloned.1.call-start = ((), (), s32[]{:S(2)}) async-start(), calls=%async_computation | async-start | bytes 5242880 | tf_op jit(solution)/shard_map/all_gather | solution.py:24
  9.6 80.7 %all-gather.9.cloned.1.call-start = ((), (), s32[]{:S(2)}) async-start(), calls=%async_computation.1 | async-start | bytes 3932160 | tf_op jit(solution)/shard_map/all_gather | solution.py:24
  11.8 99.7 %all-gather.11.cloned.1.call-start = ((), (), s32[]{:S(2)}) async-start(), calls=%async_computation.2 | async-start | bytes 2621440 | tf_op jit(solution)/shard_map/all_gather | solution.py:24
  13.8 113.0 %all-gather.13.cloned.1.call-start = ((), (), s32[]{:S(2)}) async-start(), calls=%async_computation.3 | async-start | bytes 1310720 | tf_op jit(solution)/shard_map/all_gather | solution.py:24
Sparse Core Ops, SparseCore 0:
  8.8 19.8 all-gather.14
  30.2 32.7 all-gather.6
  64.5 25.8 all-gather.8
  91.7 19.7 all-gather.10
  112.9 13.8 all-gather.12
where the time goes:
time: 137 us; the launch traced here: 136 us
  waiting for transfers between devices  102 us (74%)
  between operations  13.2 us (10%)
  matrix products  10.3 us (8%)
  local copies, waits for them, and re-layouts  9.38 us (7%)
    all_gather x4, waiting for transfers between devices, local_product(): panels = lax.all_gather(panel, 'col', axis=1, tiled=True)  88.1 us
    all_gather x1, waiting for transfers between devices, local_product(): gathered_rhs = lax.all_gather(rhs_loc, 'row', axis=0)  13.2 us
    dot_general x4, matrix products, local_product(): jnp.dot(panels, rhs_steps[step], preferred_element_type=jnp.float32)  10.3 us
    slice x4, local copies, waits for them, and re-layouts, local_product(): panel = lower_loc[first_row:, step * BLOCK_SIZE:(step + 1) * BLOCK_SIZE]  7.98 us
  transfers between devices with their start and end apart: 5, of which 5 were waited for; matrix products, arithmetic and copies ran while one was open for 13% of the time, Pallas kernels for 0%

commit v1 on v0

v1 whole, which is shorter than its diff:
```python
import jax
import jax.numpy as jnp
from jax import lax
from jax.experimental import pallas as pl
from jax.experimental.pallas import tpu as pltpu
from jax.sharding import PartitionSpec as P

BLK = 256
RB = 8
CB = 4
MESH = pl.DeviceIdType.MESH


def kernel(l_hbm, b_hbm, out, lb, bs, bo, bc, bx, xl, own, psend, precv, x0,
           loc_sem, sxb, rxb, syo, ryo, sfw, rfw, spl, rpl, smx, rmx, sp, rp):
    r = lax.axis_index("row")
    col = lax.axis_index("col")
    x = col // 2
    core = col % 2
    xn = {"col": col + 2 - 4 * x}
    yn = {"row": 1 - r}
    pn = {"col": col + 1 - 2 * core}

    def rows(i, n=1):
        return pl.ds(i * BLK, n * BLK)

    def remote(src, dst, ssem, rsem, dev):
        return pltpu.make_async_remote_copy(
            src_ref=src, dst_ref=dst, send_sem=ssem, recv_sem=rsem, device_id=dev, device_id_type=MESH)

    barrier = pltpu.get_barrier_semaphore()
    for dev in (xn, yn, pn):
        pl.semaphore_signal(barrier, inc=1, device_id=dev, device_id_type=MESH)

    loads = []
    for t in range(CB):
        loads.append((b_hbm.at[rows(2 * t + 1 - x)], bs.at[rows(t)]))
    for t in range(CB):
        loads.append((b_hbm.at[rows(2 * t + x)], bo.at[r, rows(t)]))
    loads.append((b_hbm.at[rows(1 - x)], bx.at[r]))
    for u in range(CB):
        part = (rows(2 * u, 2), pl.ds(0, (u + 1) * BLK))
        loads.append((l_hbm.at[part], lb.at[(core,) + part]))
    loads = [pltpu.make_async_copy(s, d, loc_sem.at[i]) for i, (s, d) in enumerate(loads)]
    for cp in loads:
        cp.start()
    for cp in loads:
        cp.wait()

    x_b = [remote(bs.at[rows(t)], bc.at[r, rows(t)], sxb.at[t], rxb.at[t], xn) for t in range(CB)]
    y_own = [remote(bo.at[r, rows(t)], bo.at[r, rows(t)], syo.at[t], ryo.at[t], yn) for t in range(CB)]
    y_bx = remote(bx.at[r], bx.at[r], syo.at[CB], ryo.at[CB], yn)
    y_fwd = [remote(bc.at[r, rows(t)], bc.at[r, rows(t)], sfw.at[t], rfw.at[t], yn) for t in range(CB)]
    p_l = []
    for u in range(CB):
        part = (core, rows(2 * u, 2), pl.ds(0, (u + 1) * BLK))
        p_l.append(remote(lb.at[part], lb.at[part], spl.at[u], rpl.at[u], pn))
    x_l = [remote(lb.at[core, rows(j + 1), pl.ds(0, BLK)], xl.at[core, j], smx.at[j], rmx.at[j], xn) for j in range(2)]
    p_xl = [remote(xl.at[core, j], xl.at[core, j], smx.at[2 + j], rmx.at[2 + j], pn) for j in range(2)]
    x_0 = remote(x0.at[0], x0.at[1], smx.at[4], rmx.at[4], xn)
    x_p = {s: remote(psend.at[s - 2], precv.at[s - 2], sp.at[s - 2], rp.at[s - 2], xn) for s in range(2, RB)}

    left = x == 0
    right = x == 1
    sends_l1 = (r == 1) | (x == 0) | (core == 0)
    gets_l1 = (r == 1) | (x == 1) | (core == 0)
    partner_gets_l1 = (r == 1) | (x == 1) | (core == 1)

    pl.semaphore_wait(barrier, 3)

    for cp in x_b + y_own[:3] + p_l:
        cp.start()
    pl.when(sends_l1)(x_l[0].start)
    pl.when(right)(x_l[1].start)

    for t in range(CB):
        x_b[t].wait_recv()
        y_fwd[t].start()
        if t == 2:
            y_own[3].start()
    y_bx.start()

    def product(s, cross):
        k = (s // 2 + 1) * BLK
        total = None
        for p in range(2):
            rhs = bo[p, :k, :]
            if cross:
                rhs = jnp.concatenate([rhs, bc[p, :k, :]], axis=1)
            term = jnp.dot(lb[p, s * BLK:(s + 1) * BLK, :k], rhs, preferred_element_type=jnp.float32)
            total = term if total is None else total + term
        return total

    for t in range(CB):
        y_own[t].wait_recv()
        y_fwd[t].wait_recv()
        p_l[t].wait_recv()
        for s in (2 * t, 2 * t + 1):
            if s == 0:
                @pl.when(left)
                def _():
                    total = product(0, True)
                    x0[0, :, :] = total[:, 128:].astype(jnp.bfloat16)
                    out[0:BLK, :] = total[:, :128].astype(jnp.bfloat16)
                    x_0.start()
            elif s == 1:
                own[1] = product(1, False)
            else:
                total = product(s, True)
                psend[s - 2] = total[:, 128:]
                own[s] = total[:, :128]
                if s == 2:
                    pl.when(left)(x_p[s].start)
                else:
                    x_p[s].start()

    @pl.when(gets_l1)
    def _():
        x_l[0].wait_recv()
        p_xl[0].start()

    @pl.when(left)
    def _():
        x_l[1].wait_recv()
        p_xl[1].start()

    y_bx.wait_recv()
    pl.when(partner_gets_l1)(p_xl[0].wait_recv)

    @pl.when((r == 1) | right)
    def _():
        own[1] += jnp.dot(xl[1, 0], bx[1], preferred_element_type=jnp.float32)

    out[BLK:2 * BLK, :] = (own[1] + jnp.dot(xl[0, 0], bx[0], preferred_element_type=jnp.float32)).astype(jnp.bfloat16)

    @pl.when(left)
    def _():
        p_xl[1].wait_recv()
        total = own[2]
        for p in range(2):
            total += jnp.dot(xl[p, 1], bx[p], preferred_element_type=jnp.float32)
        out[2 * BLK:3 * BLK, :] = total.astype(jnp.bfloat16)

    @pl.when(right)
    def _():
        x_0.wait_recv()
        out[0:BLK, :] = x0[1]
        x_p[2].wait_recv()
        out[2 * BLK:3 * BLK, :] = (own[2] + precv[0]).astype(jnp.bfloat16)

    for s in range(3, RB):
        x_p[s].wait_recv()
        out[s * BLK:(s + 1) * BLK, :] = (own[s] + precv[s - 2]).astype(jnp.bfloat16)

    for cp in x_b + y_own + [y_bx] + y_fwd + p_l + [x_p[s] for s in range(3, RB)]:
        cp.wait_send()
    pl.when(sends_l1)(x_l[0].wait_send)
    pl.when(gets_l1)(p_xl[0].wait_send)
    pl.when(right)(x_l[1].wait_send)

    @pl.when(left)
    def _():
        p_xl[1].wait_send()
        x_0.wait_send()
        x_p[2].wait_send()


def solution(mesh):
    def local_product(lower_loc, rhs_loc):
        n_rows, cols = rhs_loc.shape
        depth = lower_loc.shape[1]
        bf, f32 = jnp.bfloat16, jnp.float32
        dma = pltpu.SemaphoreType.DMA
        return pl.pallas_call(
            kernel,
            out_shape=jax.ShapeDtypeStruct((n_rows, cols), bf),
            in_specs=[pl.BlockSpec(memory_space=pltpu.HBM)] * 2,
            out_specs=pl.BlockSpec(memory_space=pltpu.VMEM),
            scratch_shapes=[
                pltpu.VMEM((2, n_rows, depth), bf),
                pltpu.VMEM((depth, cols), bf),
                pltpu.VMEM((2, depth, cols), bf),
                pltpu.VMEM((2, depth, cols), bf),
                pltpu.VMEM((2, BLK, cols), bf),
                pltpu.VMEM((2, 2, BLK, BLK), bf),
                pltpu.VMEM((RB, BLK, cols), f32),
                pltpu.VMEM((RB - 2, BLK, cols), f32),
                pltpu.VMEM((RB - 2, BLK, cols), f32),
                pltpu.VMEM((2, BLK, cols), bf),
                dma((3 * CB + 1,)),
                dma((CB,)), dma((CB,)),
                dma((CB + 1,)), dma((CB + 1,)),
                dma((CB,)), dma((CB,)),
                dma((CB,)), dma((CB,)),
                dma((5,)), dma((5,)),
                dma((RB - 2,)), dma((RB - 2,)),
            ],
            compiler_params=pltpu.CompilerParams(
                collective_id=0, has_side_effects=True, vmem_limit_bytes=32 * 2**20),
        )(lower_loc, rhs_loc)

    return jax.shard_map(local_product, mesh=mesh, in_specs=(P("row", "col"), P("row", ("batch", "col"))), out_specs=P("row", ("batch", "col")), check_vma=False)
```

time: 137 us -> 34.8 us (0.25)
  the two profiles are of different devices: /device:TPU:1 before, /device:TPU:0 now
where the time goes in v1:
time: 34.8 us; the launch traced here: 34.6 us
  Pallas kernels  30.6 us (88%)
  local copies, waits for them, and re-layouts  4.02 us (12%)
    pallas_call x1, Pallas kernels, local_product(): pl.pallas_call(kernel, out_shape=jax.ShapeDtypeStruct((n_rows, cols), bf)...  30.6 us
    unnamed x5, local copies, waits for them, and re-layouts  4.02 us

profile of v1, /device:TPU:0, one launch (start us, length us, event | category | flops | bytes accessed | tf_op | source)
XLA Modules:
  0.0 34.6 jit_solution(3778246136165200584)
XLA Ops:
  0.0 0.0 copy-start
  0.0 2.2 %copy-done = bf16[2048,1024]{1,0:T(8,128)(2,1)S(1)} copy-done((bf16[2048,1024]{1,0:T(8,128)(2,1)S(1)}, bf16[2048,1024]{1,0:T(8,128)(2,1)}, u32[]{:S(2)}) %copy-start) | copy-done | bytes 4194328
  2.2 0.0 copy-start.1
  2.2 1.0 %copy-done.1 = bf16[2048,128]{1,0:T(8,128)(2,1)S(1)} copy-done((bf16[2048,128]{1,0:T(8,128)(2,1)S(1)}, bf16[2048,128]{1,0:T(8,128)(2,1)}, u32[]{:S(2)}) %copy-start.1) | copy-done | bytes 524312
  3.2 30.6 %shard_map.28 = bf16[2048,128]{1,0:T(8,128)(2,1)S(1)} custom-call(bf16[2048,1024]{1,0:T(8,128)(2,1)S(1)} %copy-done, bf16[2048,128]{1,0:T(8,128)(2,1)S(1)} %copy-done.1), custom_call_target="tpu_custom_call" | custom-call | tf_op jit(solution)/shard_map/pallas_call | solution.py:174
  33.8 0.8 %copy.4 = bf16[2048,128]{1,0:T(8,128)(2,1)} copy(bf16[2048,128]{1,0:T(8,128)(2,1)S(1)} %shard_map.28) | data formatting | bytes 1048576
Async XLA Ops:
  0.0 2.2 %copy-start = (bf16[2048,1024]{1,0:T(8,128)(2,1)S(1)}, bf16[2048,1024]{1,0:T(8,128)(2,1)}, u32[]{:S(2)}) copy-start(bf16[2048,1024]{1,0:T(8,128)(2,1)} %l_hbm.1) | copy-start | bytes 12582916
  2.2 1.0 %copy-start.1 = (bf16[2048,128]{1,0:T(8,128)(2,1)S(1)}, bf16[2048,128]{1,0:T(8,128)(2,1)}, u32[]{:S(2)}) copy-start(bf16[2048,128]{1,0:T(8,128)(2,1)} %b_hbm.1) | copy-start | bytes 1572868
